TPU v7x, 32 devices: a whole 2x2x4 slice. The times are simulated.
32 devices in a mesh: strip: 8 (over z, y), chan: 4 (over x, core).
Axes of the slice: x: 2, y: 2, z: 4, core: 2. Of those that a mesh axis runs over, the one named last changes fastest.
Arguments:
- activations: bfloat16 [64, 128, 1280], P('strip', None, 'chan'), may hold values from -17 to 17
- weight: bfloat16 [9, 1280, 1280], P(None, None, 'chan'), may hold values from -0.0546875 to 0.0546875
- gamma: float32 [1280], replicated, may hold values from 0.25 to 1.75
- beta: float32 [1280], replicated, may hold values from -3 to 3
- group_map: int32 [1280], replicated, may hold values from 0 to 31, as said below
- lengths: int32 [8], P('strip'), may hold values from 1 to 8, 48 in all
- stale_edges: bfloat16 [16, 128, 1280], P('strip', None, 'chan'), may hold values from -6 to 6
- stale_mean: float32 [32], replicated, may hold values from -0.5 to 0.5
- stale_square: float32 [32], replicated, may hold values from 1 to 4
- old_mean: float32 [8, 32], P('strip'), may hold values from -0.5 to 0.5
- old_square: float32 [8, 32], P('strip'), may hold values from 0.5 to 6
Outputs:
- upsampled: bfloat16 [128, 256, 1280], P('strip', None, 'chan')
- new_mean: float32 [32], replicated
- new_square: float32 [32], replicated
Inputs may be any that keep to these rules, and one draw needn't show every extreme that they name: `group_map`: every group has exactly 40 channels. The lengths sum to 48, and some strip uses all 8 rows.
All inputs are finite; a program needn't handle non-finite values. No bound on the sum of `lengths` on one device may be relied on, other than what follows from the above.
Results may differ from a plain program's by a relative error of at most 0.0027.
Values may be sent and summed in bfloat16 or wider, within the bound.
A program may use at most 64 MiB of HBM per device.

v0:
```python
import jax
import jax.numpy as jnp
from jax import lax
from jax.sharding import PartitionSpec as P

EPS = 1e-05


def padded_2(block, sides, width):
    for axis, dim in sides:
        count = lax.axis_size(axis)
        forward = [(i, i + 1) for i in range(count - 1)]
        backward = [(target, source) for source, target in forward]
        low = lax.ppermute(
            lax.slice_in_dim(block, block.shape[dim] - width, None, axis=dim), axis, forward
        )
        high = lax.ppermute(lax.slice_in_dim(block, 0, width, axis=dim), axis, backward)
        block = jnp.concatenate([low, block, high], axis=dim)
    return block


def per_device(
    activations,
    weight,
    gamma,
    beta,
    group_map,
    lengths,
    stale_edges,
    stale_mean,
    stale_square,
    old_mean,
    old_square,
):
    rows, width, local_c = activations.shape
    channels = weight.shape[1]
    groups = stale_mean.shape[0]
    per_group = channels // groups
    offset = lax.axis_index("chan") * local_c
    member = (group_map[:, None] == jnp.arange(groups, dtype=jnp.int32)[None, :]).astype(
        jnp.float32
    )
    local_member = lax.dynamic_slice_in_dim(member, offset, local_c, 0)
    length = lengths[0]
    used = (jnp.arange(rows, dtype=jnp.int32) < length).astype(jnp.float32)[:, None, None]
    values = activations.astype(jnp.float32) * used
    chan_sum = jnp.sum(values, axis=(0, 1))
    chan_sq = jnp.sum(values * values, axis=(0, 1))
    part_one = jnp.sum(chan_sum[:, None] * local_member, axis=0)
    part_two = jnp.sum(chan_sq[:, None] * local_member, axis=0)
    strip_one, strip_two = lax.psum((part_one, part_two), "chan")
    total_count = float(lax.axis_size("strip") * (3 * rows // 4) * width * per_group)
    image_one, image_two = lax.psum((strip_one, strip_two), "strip")
    new_mean = image_one / total_count
    new_square = image_two / total_count
    count = length.astype(jnp.float32) * (width * per_group)
    fresh_mean = strip_one / count
    fresh_square = strip_two / count
    mean_g = stale_mean + fresh_mean - old_mean[0]
    square_g = stale_square + fresh_square - old_square[0]
    var_g = jnp.maximum(square_g - mean_g * mean_g, 0.5 * (fresh_square - fresh_mean * fresh_mean))
    rstd_g = lax.rsqrt(var_g + EPS)
    scale_c = jnp.sum(member * rstd_g[None, :], axis=1) * gamma
    shift_c = beta - jnp.sum(member * mean_g[None, :], axis=1) * scale_c
    bordered = padded_2(stale_edges, (("strip", 0),), 1)
    bounds = jnp.stack([bordered[0], bordered[3]], axis=0)
    initial = jnp.zeros((rows * width, local_c), jnp.float32)
    total = initial
    piece = lax.all_gather(activations, "chan", axis=2, tiled=True)
    bound = lax.all_gather(bounds, "chan", axis=2, tiled=True)
    depth = piece.shape[2]
    act = (jax.nn.silu(piece.astype(jnp.float32) * scale_c + shift_c) * used).astype(jnp.bfloat16)
    padded = jnp.concatenate([bound[0:1], act, jnp.zeros((1, width, depth), jnp.bfloat16)], axis=0)
    place = (jnp.arange(rows + 2, dtype=jnp.int32) == length + 1)[:, None, None]
    padded = jnp.where(place, bound[1][None], padded)
    padded = jnp.pad(padded, ((0, 0), (1, 1), (0, 0)))
    for tap in range(9):
        down, across = (tap // 3, tap % 3)
        patch = padded[down : down + rows, across : across + width].reshape(rows * width, depth)
        total = total + jnp.dot(patch, weight[tap], preferred_element_type=jnp.float32)
    block = ((activations.astype(jnp.float32) + total.reshape(rows, width, local_c)) * used).astype(
        jnp.bfloat16
    )
    upsampled = jnp.repeat(jnp.repeat(block, 2, axis=0), 2, axis=1)
    return (upsampled, new_mean, new_square)


def solution(mesh):
    in_specs = (
        P("strip", None, "chan"),
        P(None, None, "chan"),
        P(),
        P(),
        P(),
        P("strip"),
        P("strip", None, "chan"),
        P(),
        P(),
        P("strip", None),
        P("strip", None),
    )
    out_specs = (P("strip", None, "chan"), P(), P())
    return jax.shard_map(
        per_device, mesh=mesh, in_specs=in_specs, out_specs=out_specs, check_vma=False
    )
```

profile of v0, /device:TPU:0, one launch (start us, length us, event | category | flops | bytes accessed | tf_op | source)
XLA Modules:
  0.0 100.3 jit_solution(1135148588902950023)
XLA Ops:
  7.3 2.4 %copy.49 = bf16[8,128,320]{1,0,2:T(8,128)(2,1)} copy(bf16[8,128,320]{1,2,0:T(8,128)(2,1)} %param.11) | data formatting | bytes 1310720 | tf_op args[0]
  9.7 0.9 fusion.30
  10.8 1.3 %collective-permute-start.1 = (bf16[1,128,320]{1,0,2:T(2,128)(2,1)S(1)}, bf16[1,128,320]{1,0,2:T(2,128)(2,1)S(1)}, u32[]{:S(2)}, u32[]{:S(2)}) collective-permute-start(bf16[1,128,320]{1,0,2:T(2,128)(2,1)S(1)} %copy.55), channel_id=1, source_target_pairs={{4,0},{8,4},{12,8},{16,12},{20,16},{24,20},{28,24},{5,1},{9,5},{13... | collective-permute-start | bytes 245768 | tf_op jit(solution)/shard_map/ppermute | solution.py:17
  12.2 5.5 %collective-permute-start = (bf16[1,128,320]{1,0,2:T(2,128)(2,1)S(1)}, bf16[1,128,320]{1,0,2:T(2,128)(2,1)S(1)}, u32[]{:S(2)}, u32[]{:S(2)}) collective-permute-start(bf16[1,128,320]{1,0,2:T(2,128)(2,1)S(1)} %copy.54), channel_id=1, source_target_pairs={{0,4},{4,8},{8,12},{12,16},{16,20},{20,24},{24,28},{1,5},{5,9},{9,... | collective-permute-start | bytes 245768 | tf_op jit(solution)/shard_map/ppermute | solution.py:14
  18.5 0.4 fusion.3
  18.9 0.2 fusion.26
  19.1 7.3 %all-reduce.2 = (f32[32]{0:T(128)S(1)}, f32[32]{0:T(128)S(1)}) all-reduce(f32[32]{0:T(128)S(1)} %get-tuple-element.21, f32[32]{0:T(128)S(1)} %get-tuple-element.20), channel_id=1, replica_groups=mesh['strip'=8,'chan'=4] {'chan'}, use_global_device_ids=true, to_apply=%region_5.0 | all-reduce | flops 64 | bytes 512 | tf_op jit(solution)/shard_map/psum | solution.py:51
  26.5 19.8 %all-reduce.1 = (f32[32]{0:T(128)S(1)}, f32[32]{0:T(128)S(1)}) all-reduce(f32[32]{0:T(128)S(1)} %get-tuple-element.26, f32[32]{0:T(128)S(1)} %get-tuple-element.27), channel_id=1, replica_groups=mesh['strip'=8,'chan'=4] {'strip'}, use_global_device_ids=true, to_apply=%region_8.0 | all-reduce | flops 64 | bytes 512 | tf_op jit(solution)/shard_map/psum | solution.py:53
  46.4 0.5 broadcast_multiply_fusion
  47.0 0.4 pad_maximum_fusion
  47.3 7.5 %all_gather.6 = bf16[2,128,1280]{1,0,2:T(2,128)(2,1)S(1)} all-gather(bf16[2,128,320]{1,0,2:T(2,128)(2,1)S(1)} %pad_maximum_fusion), channel_id=1, replica_groups=mesh['strip'=8,'chan'=4] {'chan'}, dimensions={2}, use_global_device_ids=true | all-gather | bytes 819200 | tf_op jit(solution)/shard_map/all_gather | solution.py:70
  54.9 0.9 fusion.29
  55.8 1.1 %copy.56 = bf16[1,128,1280]{2,1,0:T(8,128)(2,1)} copy(bf16[1,128,1280]{1,0,2:T(2,128)(2,1)S(1)} %get-tuple-element.41) | data formatting | bytes 655360
  56.9 1.1 %copy.57 = bf16[1,128,1280]{2,1,0:T(8,128)(2,1)} copy(bf16[1,128,1280]{1,0,2:T(2,128)(2,1)S(1)} %get-tuple-element.42) | data formatting | bytes 655360
  58.0 3.8 %copy.50 = bf16[8,128,1280]{2,1,0:T(8,128)(2,1)S(1)} copy(bf16[8,128,1280]{1,0,2:T(8,128)(2,1)} %all-gather.2.cloned.1.call-done) | data formatting | bytes 5242880 | tf_op jit(solution)/shard_map/all_gather | solution.py:69
  61.9 1.7 %multiply_convert_fusion = bf16[8,128,1280]{2,1,0:T(8,128)(2,1)S(1)} fusion(bf16[8,128,1280]{2,1,0:T(8,128)(2,1)S(1)} %copy.50, f32[8]{0:T(128)S(1)} %compare_convert_fusion, f32[1280]{0:T(1024)S(1)} %get-tuple-element.28, f32[1280]{0:T(1024)S(1)} %get-tuple-element.29), kind=kLoop, calls=%fused_computation | loop fusion | flops 11796480 | bytes 5253152 | tf_op jit(solution)/shard_map/convert_element_type | solution.py:72
  63.5 0.4 maximum_select_fusion
  64.0 10.0 %pad_slice_fusion = (bf16[8,128,1280]{2,1,0:T(8,128)(2,1)S(1)}, bf16[8,128,1280]{2,1,0:T(8,128)(2,1)S(1)}, bf16[8,128,1280]{2,1,0:T(8,128)(2,1)S(1)}, bf16[8,128...) fusion(bf16[10,128,1280]{2,1,0:T(8,128)(2,1)S(1)} %maximum_sele, ...), kind=kLoop, calls=%fused_computation.2 | loop fusion | bytes 34734080 | tf_op jit(solution)/shard_map/slice | solution.py:79
  74.1 2.3 %fusion.14 = f32[1024,320]{0,1:T(8,128)S(1)} fusion(bf16[1024,1280]{1,0:T(8,128)(2,1)S(1)} %bitcast.78, bf16[9,1280,320]{1,2,0:T(8,128)(2,1)} %param.12), kind=kOutput, calls=%fused_computation.32 | convolution fusion | flops 838860800 | bytes 4751360 | tf_op jit(solution)/shard_map/dot_general | solution.py:80
  76.4 2.3 %convolution_add_fusion.7 = f32[1024,320]{0,1:T(8,128)S(1)} fusion(f32[1024,320]{0,1:T(8,128)S(1)} %fusion.14, bf16[1024,1280]{1,0:T(8,128)(2,1)S(1)} %bitcast.77, bf16[9,1280,320]{1,2,0:T(8,128)(2,1)} %param.12), kind=kOutput, calls=%fused_computation.20 | convolution fusion | flops 839188480 | bytes 6062080 | tf_op jit(solution)/shard_map/dot_general | solution.py:80
  78.8 1.1 %convolution_add_fusion.6 = f32[1024,320]{0,1:T(8,128)S(1)} fusion(f32[1024,320]{0,1:T(8,128)S(1)} %convolution_add_fusion.7, bf16[1024,1280]{1,0:T(8,128)(2,1)S(1)} %bitcast.76, bf16[9,1280,320]{1,2,0:T(8,128)(2,1)S(1)} %bitcast.81), kind=kOutput, calls=%fused_computation.19 | convolution fusion | flops 839188480 | bytes 6062080 | tf_op jit(solution)/shard_map/dot_general | solution.py:80
  79.9 1.0 %convolution_add_fusion.5 = f32[1024,320]{0,1:T(8,128)S(1)} fusion(f32[1024,320]{0,1:T(8,128)S(1)} %convolution_add_fusion.6, bf16[1024,1280]{1,0:T(8,128)(2,1)S(1)} %bitcast.75, bf16[9,1280,320]{1,2,0:T(8,128)(2,1)S(1)} %bitcast.81), kind=kOutput, calls=%fused_computation.18 | convolution fusion | flops 839188480 | bytes 6062080 | tf_op jit(solution)/shard_map/dot_general | solution.py:80
  80.9 1.1 %convolution_add_fusion.4 = f32[1024,320]{0,1:T(8,128)S(1)} fusion(f32[1024,320]{0,1:T(8,128)S(1)} %convolution_add_fusion.5, bf16[1024,1280]{1,0:T(8,128)(2,1)S(1)} %bitcast.74, bf16[9,1280,320]{1,2,0:T(8,128)(2,1)S(1)} %bitcast.81), kind=kOutput, calls=%fused_computation.17 | convolution fusion | flops 839188480 | bytes 6062080 | tf_op jit(solution)/shard_map/dot_general | solution.py:80
  82.0 1.1 %convolution_add_fusion.3 = f32[1024,320]{0,1:T(8,128)S(1)} fusion(f32[1024,320]{0,1:T(8,128)S(1)} %convolution_add_fusion.4, bf16[1024,1280]{1,0:T(8,128)(2,1)S(1)} %bitcast.73, bf16[9,1280,320]{1,2,0:T(8,128)(2,1)S(1)} %bitcast.81), kind=kOutput, calls=%fused_computation.16 | convolution fusion | flops 839188480 | bytes 6062080 | tf_op jit(solution)/shard_map/dot_general | solution.py:80
  83.0 1.1 %convolution_add_fusion.2 = f32[1024,320]{0,1:T(8,128)S(1)} fusion(f32[1024,320]{0,1:T(8,128)S(1)} %convolution_add_fusion.3, bf16[1024,1280]{1,0:T(8,128)(2,1)S(1)} %bitcast.72, bf16[9,1280,320]{1,2,0:T(8,128)(2,1)S(1)} %bitcast.81), kind=kOutput, calls=%fused_computation.15 | convolution fusion | flops 839188480 | bytes 6062080 | tf_op jit(solution)/shard_map/dot_general | solution.py:80
  84.1 1.1 %convolution_add_fusion.1 = f32[1024,320]{0,1:T(8,128)S(1)} fusion(f32[1024,320]{0,1:T(8,128)S(1)} %convolution_add_fusion.2, bf16[1024,1280]{1,0:T(8,128)(2,1)S(1)} %bitcast.71, bf16[9,1280,320]{1,2,0:T(8,128)(2,1)S(1)} %bitcast.81), kind=kOutput, calls=%fused_computation.14 | convolution fusion | flops 839188480 | bytes 6062080 | tf_op jit(solution)/shard_map/dot_general | solution.py:80
  85.2 1.1 %fusion.2 = f32[40,8,8,128]{3,2,1,0:T(8,128)S(1)} fusion(f32[1024,320]{0,1:T(8,128)S(1)} %convolution_add_fusion.1, bf16[1024,1280]{1,0:T(8,128)(2,1)S(1)} %bitcast.70, bf16[9,1280,320]{1,2,0:T(8,128)(2,1)S(1)} %bitcast.81), kind=kOutput, calls=%fused_computation.13 | convolution fusion | flops 839188480 | bytes 6062080 | tf_op jit(solution)/shard_map/dot_general | solution.py:80
  86.2 0.2 fusion.5
  86.5 0.2 broadcast_in_dim.41
  86.7 1.9 %copy.52 = bf16[16,128,320]{2,0,1:T(8,128)(2,1)} copy(bf16[16,128,320]{1,2,0:T(8,128)(2,1)S(1)} %bitcast.69) | data formatting | bytes 2621440 | tf_op jit(solution)/shard_map/reshape | solution.py:84
  88.6 1.7 %broadcast_in_dim.42 = bf16[16,128,2,320]{3,0,2,1:T(8,128)(2,1)S(1)} broadcast(bf16[16,128,320]{2,0,1:T(8,128)(2,1)} %copy.52), dimensions={0,1,3} | broadcast | bytes 3932160 | tf_op jit(solution)/shard_map/broadcast_in_dim | solution.py:84
  90.3 3.1 %copy.53 = bf16[16,256,320]{1,2,0:T(8,128)(2,1)} copy(bf16[16,256,320]{2,0,1:T(8,128)(2,1)S(1)} %bitcast.68) | data formatting | bytes 5242880
  (39 shorter events, 0.6 us)
Async XLA Ops:
  7.2 11.4 %copy-start = (bf16[8,128,320]{1,2,0:T(8,128)(2,1)S(1)}, bf16[8,128,320]{1,2,0:T(8,128)(2,1)}, u32[]{:S(2)}) copy-start(bf16[8,128,320]{1,2,0:T(8,128)(2,1)} %param.11) | copy-start | bytes 1966084
  7.2 11.7 %copy-start.3 = (s32[1280]{0:T(1024)S(1)}, s32[1280]{0:T(1024)}, u32[]{:S(2)}) copy-start(s32[1280]{0:T(1024)} %param.15) | copy-start | bytes 15364
  7.2 39.0 %copy-start.6 = (f32[1,32]{1,0:T(1,128)S(1)}, f32[1,32]{1,0:T(1,128)}, u32[]{:S(2)}) copy-start(f32[1,32]{1,0:T(1,128)} %param.21) | copy-start | bytes 388
  7.2 39.0 %copy-start.8 = (f32[1,32]{1,0:T(1,128)S(1)}, f32[1,32]{1,0:T(1,128)}, u32[]{:S(2)}) copy-start(f32[1,32]{1,0:T(1,128)} %param.20) | copy-start | bytes 388
  7.2 39.0 %copy-start.7 = (f32[32]{0:T(128)S(1)}, f32[32]{0:T(128)}, u32[]{:S(2)}) copy-start(f32[32]{0:T(128)} %param.19) | copy-start | bytes 388
  7.2 39.0 %copy-start.9 = (f32[32]{0:T(128)S(1)}, f32[32]{0:T(128)}, u32[]{:S(2)}) copy-start(f32[32]{0:T(128)} %param.18) | copy-start | bytes 388
  7.2 39.7 %copy-start.4 = (f32[1280]{0:T(1024)S(1)}, f32[1280]{0:T(1024)}, u32[]{:S(2)}) copy-start(f32[1280]{0:T(1024)} %param.14) | copy-start | bytes 15364
  7.2 39.7 %copy-start.5 = (f32[1280]{0:T(1024)S(1)}, f32[1280]{0:T(1024)}, u32[]{:S(2)}) copy-start(f32[1280]{0:T(1024)} %param.13) | copy-start | bytes 15364
  7.2 50.8 %all-gather.2.cloned.1.call-start = ((), (), s32[]{:S(2)}) async-start(), calls=%async_computation | async-start | bytes 3276800 | tf_op jit(solution)/shard_map/all_gather | solution.py:69
  10.8 36.1 %collective-permute-start.1 = (bf16[1,128,320]{1,0,2:T(2,128)(2,1)S(1)}, bf16[1,128,320]{1,0,2:T(2,128)(2,1)S(1)}, u32[]{:S(2)}, u32[]{:S(2)}) collective-permute-start(bf16[1,128,320]{1,0,2:T(2,128)(2,1)S(1)} %copy.55), channel_id=1, source_target_pairs={{4,0},{8,4},{12,8},{16,12},{20,16},{24,20},{28,24},{5,1},{9,5},{13... | collective-permute-start | bytes 245768 | tf_op jit(solution)/shard_map/ppermute | solution.py:17
  12.2 34.7 %collective-permute-start = (bf16[1,128,320]{1,0,2:T(2,128)(2,1)S(1)}, bf16[1,128,320]{1,0,2:T(2,128)(2,1)S(1)}, u32[]{:S(2)}, u32[]{:S(2)}) collective-permute-start(bf16[1,128,320]{1,0,2:T(2,128)(2,1)S(1)} %copy.54), channel_id=1, source_target_pairs={{0,4},{4,8},{8,12},{12,16},{16,20},{20,24},{24,28},{1,5},{5,9},{9,... | collective-permute-start | bytes 245768 | tf_op jit(solution)/shard_map/ppermute | solution.py:14
  61.8 1.7 %copy-start.1 = (bf16[1,128,1280]{2,1,0:T(8,128)(2,1)S(1)}, bf16[1,128,1280]{2,1,0:T(8,128)(2,1)}, u32[]{:S(2)}) copy-start(bf16[1,128,1280]{2,1,0:T(8,128)(2,1)} %copy.56) | copy-start | bytes 983044
  61.9 1.7 %copy-start.2 = (bf16[1,128,1280]{2,1,0:T(8,128)(2,1)S(1)}, bf16[1,128,1280]{2,1,0:T(8,128)(2,1)}, u32[]{:S(2)}) copy-start(bf16[1,128,1280]{2,1,0:T(8,128)(2,1)} %copy.57) | copy-start | bytes 983044
  74.1 4.7 %slice-start = ((s8[7372800]{0:T(1024)(128)(4,1)}), s8[4194304]{0:T(1024)(128)(4,1)S(1)}, s32[]{:S(2)}) async-start(s8[7372800]{0:T(1024)(128)(4,1)} %bitcast.80), calls=%async_computation.1 | async-start | bytes 8388608
  76.4 2.4 %slice-start.1 = ((s8[7372800]{0:T(1024)(128)(4,1)}), s8[3178496]{0:T(1024)(128)(4,1)S(1)}, s32[]{:S(2)}) async-start(s8[7372800]{0:T(1024)(128)(4,1)} %bitcast.80), calls=%async_computation.2 | async-start | bytes 6356992
Sparse Core Ops, SparseCore 0:
  10.2 28.4 all-gather.1
where the time goes:
time: 101 us; the launch traced here: 100 us
  blocking collectives  34.6 us (34%)
  local copies, waits for them, and re-layouts  27.7 us (27%)
  between operations  15.1 us (15%)
  matrix products  12 us (12%)
  starting transfers between devices  6.87 us (7%)
  other arithmetic  3.98 us (4%)
    psum x1, blocking collectives, per_device(): image_one, image_two = lax.psum((strip_one, strip_two), 'strip')  19.8 us
    dot_general x9, matrix products, per_device(): jnp.dot(patch, weight[tap], preferred_element_type=jnp.float32)  12 us
    slice x1, local copies, waits for them, and re-layouts, per_device(): padded[down:down + rows, across:across + width].reshape(rows * width, depth)  10 us
    unnamed x30, local copies, waits for them, and re-layouts  8.07 us
    all_gather x1, blocking collectives, per_device(): bound = lax.all_gather(bounds, 'chan', axis=2, tiled=True)  7.51 us
    psum x1, blocking collectives, per_device(): strip_one, strip_two = lax.psum((part_one, part_two), 'chan')  7.31 us
    ppermute x1, starting transfers between devices, padded_2(): lax.ppermute(lax.slice_in_dim(block, block.shape[dim] - width, None, axis...  5.54 us
    all_gather x1, local copies, waits for them, and re-layouts, per_device(): piece = lax.all_gather(activations, 'chan', axis=2, tiled=True)  3.82 us
  transfers between devices with their start and end apart: 3, of which 0 were waited for; matrix products, arithmetic and copies ran while one was open for 6% of the time, Pallas kernels for 0%

commit v1 on v0

v1 whole, which is shorter than its diff:
```python
import functools

import jax
import jax.numpy as jnp
from jax import lax
from jax.experimental import pallas as pl
from jax.experimental.pallas import tpu as pltpu
from jax.sharding import PartitionSpec as P

EPS = 1e-05
MESH = pl.DeviceIdType.MESH
F32 = jnp.float32
BF16 = jnp.bfloat16
LANES = 128
HALF = 64


def silu(v):
    return 0.5 * v * (1.0 + jnp.tanh(0.5 * v))


def lane_iota(shape):
    return lax.broadcasted_iota(jnp.int32, shape, len(shape) - 1)


def conv_kernel(
    n_strip,
    n_chan,
    total_count,
    x_hbm,
    w_hbm,
    gamma_ref,
    beta_ref,
    map_ref,
    len_ref,
    edge_hbm,
    smean_ref,
    ssq_ref,
    omean_ref,
    osq_ref,
    out_ref,
    stat_ref,
    xl,
    el,
    ws,
    wr,
    ga,
    gb,
    eb,
    pad,
    st_out,
    st_chan,
    st_strip,
    st_all,
    affine,
    local_sem,
    w_sem,
    send_sem,
    recv_sem,
    edge_send,
    stat_send,
    stat_recv,
    img_send,
    img_recv,
):
    rows, width, local_c = x_hbm.shape
    channels = w_hbm.shape[1]
    groups = smean_ref.shape[1]
    main = local_c // LANES * LANES
    slots = rows + 2
    strip = lax.axis_index("strip")
    me = lax.axis_index("chan")
    n_chips = n_chan // 2
    chip, core = me // 2, me % 2
    partner = chip * 2 + (1 - core)
    up = lax.rem(strip + 1, n_strip)
    down = lax.rem(strip + n_strip - 1, n_strip)
    others = [lax.rem(chip + d, n_chips) * 2 + core for d in range(1, n_chips)]
    sources = [lax.rem(chip + n_chips - d, n_chips) * 2 + core for d in range(1, n_chips)]
    length = len_ref[0]

    x_copy = pltpu.make_async_copy(x_hbm, xl, local_sem.at[0])
    e_copy = pltpu.make_async_copy(edge_hbm, el, local_sem.at[1])
    g_copy = pltpu.make_async_copy(
        x_hbm.at[:, :, pl.ds(0, main)], ga.at[me, pl.ds(1, rows)], local_sem.at[2]
    )
    x_copy.start()
    e_copy.start()
    g_copy.start()
    w_copies = []
    for tap in range(9):
        dy, dx = tap // 3, tap % 3
        for c in range(n_chan):
            for part in range(2):
                if part == 0:
                    src = w_hbm.at[tap, pl.ds(c * local_c, main)]
                    dst = ws.at[dx, pl.ds(dy * channels + c * main, main)]
                else:
                    src = w_hbm.at[tap, pl.ds(c * local_c + main, HALF)]
                    dst = ws.at[dx, pl.ds(dy * channels + n_chan * main + c * HALF, HALF)]
                copy = pltpu.make_async_copy(src, dst, w_sem.at[(tap * n_chan + c) * 2 + part])
                copy.start()
                w_copies.append(copy)

    barrier = pltpu.get_barrier_semaphore()
    greeted = 0
    for d in range(1, n_chan):
        peer = lax.rem(me + d, n_chan)
        pl.semaphore_signal(barrier, inc=1, device_id=(strip, peer), device_id_type=MESH)
        greeted += 1
    for d in range(1, n_strip):
        peer = lax.rem(strip + d, n_strip)
        pl.semaphore_signal(barrier, inc=1, device_id=(peer, me), device_id_type=MESH)
        greeted += 1
    for side in (up, down):
        for c in [partner] + others:
            pl.semaphore_signal(barrier, inc=1, device_id=(side, c), device_id_type=MESH)
            greeted += 1

    lane_h = lane_iota((HALF, LANES))

    def packed(ref, r):
        low = ref[r, pl.ds(0, HALF), pl.ds(main, HALF)].astype(F32)
        high = ref[r, pl.ds(HALF, HALF), pl.ds(main, HALF)].astype(F32)
        return jnp.concatenate([low, high], axis=1).astype(BF16)

    e_copy.wait()
    for k in range(2):
        eb[k] = packed(el, k)
    x_copy.wait()

    def row_sums(r, carry):
        one, two = carry
        gb[me, r + 1] = packed(xl, r)
        value = jnp.where(r < length, xl[r].astype(F32), 0.0).reshape(width // 8, 8, local_c)
        return one + jnp.sum(value, axis=0), two + jnp.sum(value * value, axis=0)

    zero = jnp.zeros((8, local_c), F32)
    one, two = lax.fori_loop(0, rows, row_sums, (zero, zero))
    one = jnp.sum(one, axis=0, keepdims=True)
    two = jnp.sum(two, axis=0, keepdims=True)
    gmap = jnp.broadcast_to(map_ref[...].astype(F32), (8, channels))
    own_map = pltpu.roll(gmap, lax.rem(channels - me * local_c, channels), 1)[0:1, 0:local_c]
    group_id = lax.broadcasted_iota(jnp.int32, (groups, local_c), 0).astype(F32)
    member = (own_map == group_id).astype(F32)
    col_one = jnp.sum(member * one, axis=1, keepdims=True)
    col_two = jnp.sum(member * two, axis=1, keepdims=True)
    eye = (
        lax.broadcasted_iota(jnp.int32, (groups, LANES), 0) == lane_iota((groups, LANES))
    ).astype(F32)
    sub8 = lax.broadcasted_iota(jnp.int32, (8, LANES), 0)

    def as_rows(a, b):
        row_a = jnp.sum(eye * a, axis=0, keepdims=True)
        row_b = jnp.sum(eye * b, axis=0, keepdims=True)
        return jnp.where(sub8 == 0, row_a, jnp.where(sub8 == 1, row_b, 0.0))

    st_out[...] = as_rows(col_one, col_two)
    g_copy.wait()
    pl.semaphore_wait(barrier, greeted)

    sends = []

    def send(src, dst, s_sem, r_sem, device):
        copy = pltpu.make_async_remote_copy(
            src_ref=src, dst_ref=dst, send_sem=s_sem, recv_sem=r_sem,
            device_id=device, device_id_type=MESH,
        )
        copy.start()
        sends.append(copy)
        return copy

    stat_copies = []
    for d in range(1, n_chan):
        peer = lax.rem(me + d, n_chan)
        stat_copies.append(
            send(st_out, st_chan.at[d], stat_send.at[d], stat_recv.at[d], (strip, peer))
        )

    for k, slot, side in ((1, 0, up), (0, slots - 1, down)):
        for kind, c in enumerate([me, partner] + others):
            send(el.at[k, :, pl.ds(0, main)], ga.at[me, slot], edge_send.at[k, kind, 0],
                 recv_sem.at[kind, slot, 0], (side, c))
            send(eb.at[k], gb.at[me, slot], edge_send.at[k, kind, 1],
                 recv_sem.at[kind, slot, 1], (side, c))
    kinds = 1 + n_chips

    def row_copies(slot, kind, c, chan):
        return (
            pltpu.make_async_remote_copy(
                src_ref=ga.at[chan, slot], dst_ref=ga.at[chan, slot],
                send_sem=send_sem.at[kind, slot, 0], recv_sem=recv_sem.at[kind, slot, 0],
                device_id=(strip, c), device_id_type=MESH),
            pltpu.make_async_remote_copy(
                src_ref=gb.at[chan, slot], dst_ref=gb.at[chan, slot],
                send_sem=send_sem.at[kind, slot, 1], recv_sem=recv_sem.at[kind, slot, 1],
                device_id=(strip, c), device_id_type=MESH),
        )

    def start_row(slot, carry):
        for kind, c in enumerate(others):
            for copy in row_copies(slot, 2 + kind, c, me):
                copy.start()
        for copy in row_copies(slot, 1, partner, me):
            copy.start()
        return carry

    lax.fori_loop(1, rows + 1, start_row, 0)

    for copy in w_copies:
        copy.wait()
    block = 256
    wide = jnp.zeros((block, HALF), F32)

    def narrow(k, carry):
        at = pl.ds(pl.multiple_of(k * block, block), block)
        parts = [ws[dx, at, pl.ds(main, HALF)].astype(F32) for dx in range(3)]
        left = jnp.concatenate([parts[0], parts[1]], axis=1)
        right = jnp.concatenate([parts[2], wide], axis=1)
        wr[at, pl.ds(0, LANES)] = left.astype(BF16)
        wr[at, pl.ds(LANES, LANES)] = right.astype(BF16)
        return carry

    lax.fori_loop(0, 3 * channels // block, narrow, 0)

    for copy in stat_copies:
        copy.wait_recv()
    st_chan[0] = st_out[...]
    strip_sum = jnp.zeros((8, LANES), F32)
    for c in range(n_chan):
        strip_sum = strip_sum + st_chan[lax.rem(me - c + n_chan, n_chan)]
    st_strip[...] = strip_sum

    def as_col(row):
        return jnp.sum(eye[:, 0:groups] * row, axis=1, keepdims=True)

    count = length.astype(F32) * (width * (channels // groups))
    fresh_mean = as_col(strip_sum[0:1, 0:groups]) / count
    fresh_sq = as_col(strip_sum[1:2, 0:groups]) / count
    mean_g = as_col(smean_ref[...]) + fresh_mean - as_col(omean_ref[...])
    sq_g = as_col(ssq_ref[...]) + fresh_sq - as_col(osq_ref[...])
    var_g = jnp.maximum(sq_g - mean_g * mean_g, 0.5 * (fresh_sq - fresh_mean * fresh_mean))
    rstd_g = lax.rsqrt(var_g + EPS)
    ids = lax.broadcasted_iota(jnp.int32, (groups, channels), 0).astype(F32)
    member_all = (gmap[0:1] == ids).astype(F32)
    scale = jnp.sum(member_all * rstd_g, axis=0, keepdims=True) * gamma_ref[...]
    shift = beta_ref[...] - jnp.sum(member_all * mean_g, axis=0, keepdims=True) * scale
    lane8 = lane_iota((8, LANES))
    for k, vector in enumerate((scale, shift)):
        vector = jnp.broadcast_to(vector, (8, channels))
        tails = []
        for c in range(n_chan):
            turned = vector if c == 0 else pltpu.roll(vector, channels - c * local_c, 1)
            affine[k, :, pl.ds(c * main, main)] = turned[:, 0:main]
            tails.append(turned[:, main:main + LANES])
        for pair in range(n_chan // 2):
            both = jnp.where(
                lane8 < HALF, tails[2 * pair], pltpu.roll(tails[2 * pair + 1], HALF, 1)
            )
            affine[k, :, pl.ds(n_chan * main + pair * LANES, LANES)] = both

    img_copies = []
    for d in range(1, n_strip):
        peer = lax.rem(strip + d, n_strip)
        img_copies.append(
            send(st_strip, st_all.at[d], img_send.at[d], img_recv.at[d], (peer, me))
        )

    def forward(slot):
        for kind, c in enumerate(sources):
            for copy in row_copies(slot, 2 + kind, c, c):
                copy.wait_recv()
            for copy in row_copies(slot, 1 + n_chips + kind, partner, c):
                copy.start()

    def arrive(slot):
        for copy in row_copies(slot, 1, partner, partner):
            copy.wait_recv()
        for kind, c in enumerate(sources):
            far = c // 2 * 2 + (1 - core)
            for copy in row_copies(slot, 1 + n_chips + kind, partner, far):
                copy.wait_recv()

    def tail_pair(slot, pair):
        even = gb[2 * pair, slot].astype(F32)
        odd = gb[2 * pair + 1, slot].astype(F32)
        top = jnp.where(lane_h < HALF, even, pltpu.roll(odd, HALF, 1))
        bottom = jnp.where(lane_h < HALF, pltpu.roll(even, HALF, 1), odd)
        return jnp.concatenate([top, bottom], axis=0)

    def pieces(slot):
        for c in range(n_chan):
            yield c * main, main, functools.partial(lambda c: ga[c, slot].astype(F32), c)
        for pair in range(n_chan // 2):
            yield (n_chan * main + pair * LANES, LANES,
                   functools.partial(tail_pair, slot, pair))

    for slot in (0, slots - 1):
        forward(slot)
    for slot in (0, slots - 1):
        for copy in row_copies(slot, 0, me, me):
            copy.wait_recv()
        arrive(slot)
    has_above = strip > 0
    has_below = strip < n_strip - 1
    for at, size, load in pieces(0):
        pad[0, :, pl.ds(at, size)] = jnp.where(has_above, load(), 0.0).astype(BF16)
    for at, size, load in pieces(slots - 1):
        below = jnp.where(has_below, load(), 0.0).astype(BF16)
        pad[slots, :, pl.ds(at, size)] = below
        pad[slots - 1, :, pl.ds(at, size)] = jnp.where(
            length + 1 == slots - 1, below.astype(F32), 0.0
        ).astype(BF16)

    def activate(slot):
        forward(slot)
        arrive(slot)
        for at, size, load in pieces(slot):
            span = pl.ds(at, size)
            v = load() * affine[0, 0:1, span] + affine[1, 0:1, span]
            act = jnp.where(slot - 1 < length, silu(v), 0.0)
            below = pad[slots, :, span].astype(F32)
            pad[slot, :, span] = jnp.where(slot == length + 1, below, act).astype(BF16)

    activate(1)
    depth = 2
    m = depth * width
    place = lax.broadcasted_iota(jnp.int32, (m, 1), 0) % width
    lane_m = lane_iota((m, LANES))
    row_of = lax.broadcasted_iota(jnp.int32, (m, 1), 0) // width

    def from_left(y):
        return jnp.where(place == 0, 0.0, pltpu.roll(y, 1, 0))

    def from_right(y):
        return jnp.where(place == width - 1, 0.0, pltpu.roll(y, m - 1, 0))

    def step(t, carry):
        activate(2 * t + 2)

        @pl.when(t < rows // depth - 1)
        def _():
            activate(2 * t + 3)

        first = depth * t
        lhs = jnp.concatenate(
            [pad[pl.ds(first + dy, depth)].reshape(m, channels) for dy in range(3)], axis=1
        )
        dot = functools.partial(jnp.dot, preferred_element_type=F32)
        total = from_left(dot(lhs, ws[0, :, pl.ds(0, main)]))
        total = total + dot(lhs, ws[1, :, pl.ds(0, main)])
        total = total + from_right(dot(lhs, ws[2, :, pl.ds(0, main)]))
        y = dot(lhs, wr[...])
        y0, y2 = y[:, 0:LANES], y[:, LANES:2 * LANES]
        tail = from_left(y0) + pltpu.roll(y0, HALF, 1) + from_right(y2)
        keep = first + row_of < length
        res = xl[pl.ds(first, depth)].reshape(m, local_c).astype(F32)
        head = jnp.where(keep, res[:, 0:main] + total, 0.0).astype(BF16)
        last = jnp.where(keep, res[:, main:local_c] + tail[:, 0:HALF], 0.0).astype(BF16)
        out_ref[pl.ds(first, depth), :, pl.ds(0, main)] = head.reshape(depth, width, main)
        out_ref[pl.ds(first, depth), :, pl.ds(main, HALF)] = last.reshape(depth, width, HALF)
        return carry

    lax.fori_loop(0, rows // depth, step, 0)

    for copy in img_copies:
        copy.wait_recv()
    st_all[0] = st_strip[...]
    image = jnp.zeros((8, LANES), F32)
    for i in range(n_strip):
        image = image + st_all[lax.rem(strip - i + n_strip, n_strip)]
    stat_ref[...] = image / total_count

    for copy in sends:
        copy.wait_send()

    def drain(slot, carry):
        for kind in range(1, 2 + n_chips - 1):
            for copy in row_copies(slot, kind, partner, me):
                copy.wait_send()
        return carry

    def drain_forward(slot, carry):
        for kind in range(1 + n_chips, 2 * n_chips):
            for copy in row_copies(slot, kind, partner, me):
                copy.wait_send()
        return carry

    lax.fori_loop(1, rows + 1, drain, 0)
    lax.fori_loop(0, slots, drain_forward, 0)


def upsample_kernel(block_ref, stat_ref, out_ref, mean_ref, square_ref):
    _, width, _ = block_ref.shape
    target = lax.broadcasted_iota(jnp.int32, (2 * width, width), 0) // 2
    source = lax.broadcasted_iota(jnp.int32, (2 * width, width), 1)
    twice = (target == source).astype(F32).astype(BF16)
    wide = jnp.dot(twice, block_ref[0], preferred_element_type=F32).astype(BF16)
    out_ref[0] = wide
    out_ref[1] = wide
    groups = mean_ref.shape[1]
    mean_ref[...] = stat_ref[0:1, 0:groups]
    square_ref[...] = stat_ref[1:2, 0:groups]


def per_device(
    n_strip,
    n_chan,
    activations,
    weight,
    gamma,
    beta,
    group_map,
    lengths,
    stale_edges,
    stale_mean,
    stale_square,
    old_mean,
    old_square,
):
    rows, width, local_c = activations.shape
    channels = weight.shape[1]
    groups = stale_mean.shape[0]
    main = local_c // LANES * LANES
    slots = rows + 2
    n_chips = n_chan // 2
    kinds = 2 * n_chips
    total_count = float(n_strip * (3 * rows // 4) * width * (channels // groups))
    vmem = pl.BlockSpec(memory_space=pltpu.VMEM)
    hbm = pl.BlockSpec(memory_space=pl.ANY)
    dma = pltpu.SemaphoreType.DMA
    block, stat = pl.pallas_call(
        functools.partial(conv_kernel, n_strip, n_chan, total_count),
        out_shape=(
            jax.ShapeDtypeStruct((rows, width, local_c), BF16),
            jax.ShapeDtypeStruct((8, LANES), F32),
        ),
        in_specs=[hbm, hbm, vmem, vmem, vmem, pl.BlockSpec(memory_space=pltpu.SMEM), hbm,
                  vmem, vmem, vmem, vmem],
        out_specs=(vmem, vmem),
        scratch_shapes=[
            pltpu.VMEM((rows, width, local_c), BF16),
            pltpu.VMEM((2, width, local_c), BF16),
            pltpu.VMEM((3, 3 * channels, local_c), BF16),
            pltpu.VMEM((3 * channels, 2 * LANES), BF16),
            pltpu.VMEM((n_chan, slots, width, main), BF16),
            pltpu.VMEM((n_chan, slots, HALF, LANES), BF16),
            pltpu.VMEM((2, HALF, LANES), BF16),
            pltpu.VMEM((slots + 1, width, channels), BF16),
            pltpu.VMEM((8, LANES), F32),
            pltpu.VMEM((n_chan, 8, LANES), F32),
            pltpu.VMEM((8, LANES), F32),
            pltpu.VMEM((n_strip, 8, LANES), F32),
            pltpu.VMEM((2, 8, channels), F32),
            dma((3,)),
            dma((9 * n_chan * 2,)),
            dma((kinds, slots, 2)),
            dma((kinds, slots, 2)),
            dma((2, 1 + n_chips, 2)),
            dma((n_chan,)),
            dma((n_chan,)),
            dma((n_strip,)),
            dma((n_strip,)),
        ],
        compiler_params=pltpu.CompilerParams(
            collective_id=0, has_side_effects=True, vmem_limit_bytes=56 * 2**20
        ),
        name="conv",
    )(
        activations,
        weight,
        gamma.reshape(1, channels),
        beta.reshape(1, channels),
        group_map.reshape(1, channels),
        lengths,
        stale_edges,
        stale_mean.reshape(1, groups),
        stale_square.reshape(1, groups),
        old_mean,
        old_square,
    )
    whole = pl.BlockSpec((1, groups), lambda r: (0, 0))
    upsampled, mean, square = pl.pallas_call(
        upsample_kernel,
        grid=(rows,),
        out_shape=(
            jax.ShapeDtypeStruct((2 * rows, 2 * width, local_c), BF16),
            jax.ShapeDtypeStruct((1, groups), F32),
            jax.ShapeDtypeStruct((1, groups), F32),
        ),
        in_specs=[
            pl.BlockSpec((1, width, local_c), lambda r: (r, 0, 0)),
            pl.BlockSpec((8, LANES), lambda r: (0, 0)),
        ],
        out_specs=(pl.BlockSpec((2, 2 * width, local_c), lambda r: (r, 0, 0)), whole, whole),
        name="upsample",
    )(block, stat)
    return upsampled, mean.reshape(groups), square.reshape(groups)


def solution(mesh):
    in_specs = (
        P("strip", None, "chan"),
        P(None, None, "chan"),
        P(),
        P(),
        P(),
        P("strip"),
        P("strip", None, "chan"),
        P(),
        P(),
        P("strip", None),
        P("strip", None),
    )
    out_specs = (P("strip", None, "chan"), P(), P())
    body = functools.partial(per_device, mesh.shape["strip"], mesh.shape["chan"])
    return jax.shard_map(
        body, mesh=mesh, in_specs=in_specs, out_specs=out_specs, check_vma=False
    )
```

time: 101 us -> 76.7 us (0.76)
  Pallas kernels: 0 us -> 48.7 us
  blocking collectives: 34.6 us -> 0 us
  between operations: 15.1 us -> 1.29 us
  matrix products: 12 us -> 0 us
  starting transfers between devices: 6.87 us -> 0 us
  other arithmetic: 3.98 us -> 0 us
  local copies, waits for them, and re-layouts: 27.7 us -> 25.2 us
    pallas_call x0 -> x2, Pallas kernels: none -> 48.7 us  [the longest x1 42.4 us: per_device(): pl.pallas_call(functools.partial(conv_kernel, n_strip, n_chan, total_coun...]
    psum x2 -> x0, blocking collectives: 27.1 us -> none  [the longest x1 19.8 us: per_device(): image_one, image_two = lax.psum((strip_one, strip_two), 'strip')]
    unnamed x30 -> x4, local copies, waits for them, and re-layouts: 8.07 us -> 21.4 us
    dot_general x9 -> x0, matrix products: 12 us -> none  [per_device(): jnp.dot(patch, weight[tap], preferred_element_type=jnp.float32)]
    slice x3 -> x0, local copies, waits for them, and re-layouts: 11.9 us -> none  [the longest x1 10 us: per_device(): padded[down:down + rows, across:across + width].reshape(rows * width, depth)]
    all_gather x1 -> x0, blocking collectives: 7.51 us -> none  [per_device(): bound = lax.all_gather(bounds, 'chan', axis=2, tiled=True)]
    ppermute x2 -> x0, starting transfers between devices: 6.83 us -> none  [the longest x1 5.54 us: padded_2(): lax.ppermute(lax.slice_in_dim(block, block.shape[dim] - width, None, axis...]
    all_gather x1 -> x0, local copies, waits for them, and re-layouts: 3.82 us -> none  [per_device(): piece = lax.all_gather(activations, 'chan', axis=2, tiled=True)]
  transfers between devices with their start and end apart: 3 -> 0, of which waited for: 0 -> 0; matrix products, arithmetic and copies ran while one was open for 6% -> 0% of each run, Pallas kernels for 0% -> 0%
where the time goes in v1:
time: 76.7 us; the launch traced here: 75.2 us
  Pallas kernels  48.7 us (63%)
  local copies, waits for them, and re-layouts  25.2 us (33%)
  between operations  1.29 us (2%)
    pallas_call x1, Pallas kernels, per_device(): pl.pallas_call(functools.partial(conv_kernel, n_strip, n_chan, total_coun...  42.4 us
    unnamed x4, local copies, waits for them, and re-layouts  21.4 us
    pallas_call x1, Pallas kernels, per_device(): pl.pallas_call(upsample_kernel, grid=(rows,), out_shape=(jax.ShapeDtypeSt...  6.22 us

profile of v1, /device:TPU:0, one launch (start us, length us, event | category | flops | bytes accessed | tf_op | source)
XLA Modules:
  0.0 75.2 jit_solution(17024686975817595849)
XLA Ops:
  1.3 1.3 %reshape.27.gamma_ref = f32[1,1280]{1,0:T(1,128)} reshape(f32[1280]{0:T(1024)} %param.13) | data formatting | bytes 10240 | tf_op jit(solution)/shard_map/reshape | solution.py:472
  2.6 1.3 %reshape.28.beta_ref = f32[1,1280]{1,0:T(1,128)} reshape(f32[1280]{0:T(1024)} %param.14) | data formatting | bytes 10240 | tf_op jit(solution)/shard_map/reshape | solution.py:473
  3.9 1.3 %reshape.29.map_ref = s32[1,1280]{1,0:T(1,128)} reshape(s32[1280]{0:T(1024)} %param.15) | data formatting | bytes 10240 | tf_op jit(solution)/shard_map/reshape | solution.py:474
  5.2 1.7 %copy.16.edge_hbm = bf16[2,128,320]{2,1,0:T(8,128)(2,1)} copy(bf16[2,128,320]{1,2,0:T(8,128)(2,1)} %param.17) | data formatting | bytes 327680 | tf_op args[6]
  6.9 2.2 %copy.14.x_hbm = bf16[8,128,320]{2,1,0:T(8,128)(2,1)} copy(bf16[8,128,320]{1,2,0:T(8,128)(2,1)} %param.11) | data formatting | bytes 1310720 | tf_op args[0]
  9.1 12.9 %copy.15.w_hbm = bf16[9,1280,320]{2,1,0:T(8,128)(2,1)} copy(bf16[9,1280,320]{1,2,0:T(8,128)(2,1)} %param.12) | data formatting | bytes 14745600 | tf_op args[1]
  22.0 42.4 %conv.1 = (bf16[8,128,320]{2,1,0:T(8,128)(2,1)}, f32[8,128]{1,0:T(8,128)}) custom-call(bf16[8,128,320]{2,1,0:T(8,128)(2,1)} %copy.14.x_hbm, bf16[9,1280,320]{2,1,0:T(8,128)(2,1)} %copy.15.w_hbm, f32[1,1280]{1,0:T(1,128)} %reshape.27.gamma_ref, f32[1,1280]{1,0:T(1,128)} %reshape.28.beta_ref, s32[1,1280]{1,0:T(1,128)} %reshape.29.map_ref, s32[1]{0:T(128)S(6)} %copy.18.len_ref, ...), custom_call_target="tpu_custom_call" | custom-call | tf_op jit(solution)/shard_map/conv/pallas_call | solution.py:432
  64.4 6.2 %upsample.1 = (bf16[16,256,320]{2,1,0:T(8,128)(2,1)}, f32[1,32]{1,0:T(1,128)}, f32[1,32]{1,0:T(1,128)}) custom-call(bf16[8,128,320]{2,1,0:T(8,128)(2,1)} %get-tuple-element.8.block_ref, f32[8,128]{1,0:T(8,128)} %get-tuple-element.9.stat_ref), custom_call_target="tpu_custom_call" | custom-call | tf_op jit(solution)/shard_map/upsample/pallas_call | solution.py:483
  70.6 4.5 %copy.17 = bf16[16,256,320]{1,2,0:T(8,128)(2,1)} copy(bf16[16,256,320]{2,1,0:T(8,128)(2,1)} %get-tuple-element.13) | data formatting | bytes 5242880

commit v2 on v1

v2 whole, which is shorter than its diff:
```python
import functools

import jax
import jax.numpy as jnp
from jax import lax
from jax.experimental import pallas as pl
from jax.experimental.pallas import tpu as pltpu
from jax.sharding import PartitionSpec as P

EPS = 1e-05
MESH = pl.DeviceIdType.MESH
F32 = jnp.float32
BF16 = jnp.bfloat16
LANES = 128


def spread(row):
    return jnp.transpose(jnp.broadcast_to(row, (LANES, LANES)))


def lane_iota(shape):
    return lax.broadcasted_iota(jnp.int32, shape, len(shape) - 1)


def conv_kernel(
    n_strip,
    n_chan,
    total_count,
    x_hbm,
    w_hbm,
    gamma_ref,
    beta_ref,
    map_ref,
    len_ref,
    edge_hbm,
    smean_ref,
    ssq_ref,
    omean_ref,
    osq_ref,
    out_ref,
    stat_ref,
    xl,
    el,
    ws,
    ga,
    pad,
    st_out,
    st_chan,
    st_strip,
    st_all,
    affine,
    local_sem,
    w_sem,
    send_sem,
    recv_sem,
    edge_send,
    stat_send,
    stat_recv,
    img_send,
    img_recv,
):
    rows, local_c, width = x_hbm.shape
    channels = w_hbm.shape[2]
    groups = smean_ref.shape[1]
    slots = rows + 2
    strip = lax.axis_index("strip")
    me = lax.axis_index("chan")
    n_chips = n_chan // 2
    chip, core = me // 2, me % 2
    partner = chip * 2 + (1 - core)
    up = lax.rem(strip + 1, n_strip)
    down = lax.rem(strip + n_strip - 1, n_strip)
    others = [lax.rem(chip + d, n_chips) * 2 + core for d in range(1, n_chips)]
    sources = [lax.rem(chip + n_chips - d, n_chips) * 2 + core for d in range(1, n_chips)]
    length = len_ref[0]

    x_copy = pltpu.make_async_copy(x_hbm, xl, local_sem.at[0])
    e_copy = pltpu.make_async_copy(edge_hbm, el, local_sem.at[1])
    g_copy = pltpu.make_async_copy(x_hbm, ga.at[me, pl.ds(1, rows)], local_sem.at[2])
    x_copy.start()
    e_copy.start()
    g_copy.start()
    w_copies = []
    for dy in range(3):
        taps = pl.ds(3 * dy, 3)
        copy = pltpu.make_async_copy(w_hbm.at[taps], ws.at[taps], w_sem.at[dy])
        copy.start()
        w_copies.append(copy)

    barrier = pltpu.get_barrier_semaphore()
    greeted = 0
    for d in range(1, n_chan):
        peer = lax.rem(me + d, n_chan)
        pl.semaphore_signal(barrier, inc=1, device_id=(strip, peer), device_id_type=MESH)
        greeted += 1
    for d in range(1, n_strip):
        peer = lax.rem(strip + d, n_strip)
        pl.semaphore_signal(barrier, inc=1, device_id=(peer, me), device_id_type=MESH)
        greeted += 1
    for side in (up, down):
        for c in [partner] + others:
            pl.semaphore_signal(barrier, inc=1, device_id=(side, c), device_id_type=MESH)
            greeted += 1

    e_copy.wait()
    x_copy.wait()

    def row_sums(r, carry):
        one, two = carry
        value = jnp.where(r < length, xl[r].astype(F32), 0.0)
        return one + value, two + value * value

    zero = jnp.zeros((local_c, width), F32)
    one, two = lax.fori_loop(0, rows, row_sums, (zero, zero))
    one = jnp.sum(one, axis=1, keepdims=True)
    two = jnp.sum(two, axis=1, keepdims=True)
    gmap = jnp.broadcast_to(map_ref[...].reshape(1, channels).astype(F32), (8, channels))
    own_map = pltpu.roll(gmap, lax.rem(channels - me * local_c, channels), 1)[0:1]
    blocks = -(-local_c // LANES)
    own_map = jnp.concatenate(
        [spread(own_map[:, k * LANES:(k + 1) * LANES]) for k in range(blocks)], axis=0
    )[0:local_c]
    member = (own_map == lane_iota((local_c, LANES)).astype(F32)).astype(F32)
    row_one = jnp.sum(member * one, axis=0, keepdims=True)
    row_two = jnp.sum(member * two, axis=0, keepdims=True)
    eye = (
        lax.broadcasted_iota(jnp.int32, (groups, LANES), 0) == lane_iota((groups, LANES))
    ).astype(F32)
    sub8 = lax.broadcasted_iota(jnp.int32, (8, LANES), 0)
    st_out[...] = jnp.where(sub8 == 0, row_one, jnp.where(sub8 == 1, row_two, 0.0))
    g_copy.wait()
    pl.semaphore_wait(barrier, greeted)

    sends = []

    def send(src, dst, s_sem, r_sem, device):
        copy = pltpu.make_async_remote_copy(
            src_ref=src, dst_ref=dst, send_sem=s_sem, recv_sem=r_sem,
            device_id=device, device_id_type=MESH,
        )
        copy.start()
        sends.append(copy)
        return copy

    stat_copies = []
    for d in range(1, n_chan):
        peer = lax.rem(me + d, n_chan)
        stat_copies.append(
            send(st_out, st_chan.at[d], stat_send.at[d], stat_recv.at[d], (strip, peer))
        )

    for k, slot, side in ((1, 0, up), (0, slots - 1, down)):
        for kind, c in enumerate([me, partner] + others):
            send(el.at[k], ga.at[me, slot], edge_send.at[k, kind],
                 recv_sem.at[kind, slot], (side, c))

    def row_copy(slot, kind, c, chan):
        return pltpu.make_async_remote_copy(
            src_ref=ga.at[chan, slot], dst_ref=ga.at[chan, slot],
            send_sem=send_sem.at[kind, slot], recv_sem=recv_sem.at[kind, slot],
            device_id=(strip, c), device_id_type=MESH,
        )

    def start_row(slot, carry):
        for kind, c in enumerate(others):
            row_copy(slot, 2 + kind, c, me).start()
        row_copy(slot, 1, partner, me).start()
        return carry

    lax.fori_loop(1, rows + 1, start_row, 0)

    for copy in stat_copies:
        copy.wait_recv()
    st_chan[0] = st_out[...]
    strip_sum = jnp.zeros((8, LANES), F32)
    for c in range(n_chan):
        strip_sum = strip_sum + st_chan[lax.rem(me - c + n_chan, n_chan)]
    st_strip[...] = strip_sum

    def as_col(row):
        return jnp.sum(eye[:, 0:groups] * row, axis=1, keepdims=True)

    count = length.astype(F32) * (width * (channels // groups))
    fresh_mean = as_col(strip_sum[0:1, 0:groups]) / count
    fresh_sq = as_col(strip_sum[1:2, 0:groups]) / count
    mean_g = as_col(smean_ref[...]) + fresh_mean - as_col(omean_ref[...])
    sq_g = as_col(ssq_ref[...]) + fresh_sq - as_col(osq_ref[...])
    var_g = jnp.maximum(sq_g - mean_g * mean_g, 0.5 * (fresh_sq - fresh_mean * fresh_mean))
    rstd_g = lax.rsqrt(var_g + EPS)
    ids = lax.broadcasted_iota(jnp.int32, (groups, channels), 0).astype(F32)
    member_all = (gmap[0:1] == ids).astype(F32)
    scale = jnp.sum(member_all * rstd_g, axis=0, keepdims=True) * gamma_ref[...].reshape(1, channels)
    shift = beta_ref[...].reshape(1, channels) - (
        jnp.sum(member_all * mean_g, axis=0, keepdims=True) * scale
    )
    for k, vector in enumerate((scale, shift)):
        for j in range(channels // LANES):
            span = slice(j * LANES, (j + 1) * LANES)
            affine[k, span, :] = spread(0.5 * vector[:, span])

    img_copies = []
    for d in range(1, n_strip):
        peer = lax.rem(strip + d, n_strip)
        img_copies.append(
            send(st_strip, st_all.at[d], img_send.at[d], img_recv.at[d], (peer, me))
        )

    def forward(slot):
        for kind, c in enumerate(sources):
            row_copy(slot, 2 + kind, c, c).wait_recv()
            row_copy(slot, 1 + n_chips + kind, partner, c).start()

    def arrive(slot):
        row_copy(slot, 1, partner, partner).wait_recv()
        for kind, c in enumerate(sources):
            far = c // 2 * 2 + (1 - core)
            row_copy(slot, 1 + n_chips + kind, partner, far).wait_recv()

    for slot in (0, slots - 1):
        forward(slot)
    for slot in (0, slots - 1):
        row_copy(slot, 0, me, me).wait_recv()
        arrive(slot)
    has_above = strip > 0
    has_below = strip < n_strip - 1
    for c in range(n_chan):
        span = pl.ds(c * local_c, local_c)
        pad[0, span] = jnp.where(has_above, ga[c, 0].astype(F32), 0.0).astype(BF16)
        below = jnp.where(has_below, ga[c, slots - 1].astype(F32), 0.0)
        pad[slots, span] = below.astype(BF16)
        pad[slots - 1, span] = jnp.where(length + 1 == slots - 1, below, 0.0).astype(BF16)

    def activate(slot):
        forward(slot)
        arrive(slot)
        for c in range(n_chan):
            span = pl.ds(c * local_c, local_c)
            h = ga[c, slot].astype(F32) * affine[0, span] + affine[1, span]
            act = jnp.where(slot - 1 < length, h + h * jnp.tanh(h), 0.0)
            below = pad[slots, span].astype(F32)
            pad[slot, span] = jnp.where(slot == length + 1, below, act).astype(BF16)

    for copy in w_copies:
        copy.wait()
    activate(1)
    depth = 2
    place = lane_iota((local_c, width))

    def from_left(y):
        return jnp.where(place == 0, 0.0, pltpu.roll(y, 1, 1))

    def from_right(y):
        return jnp.where(place == width - 1, 0.0, pltpu.roll(y, width - 1, 1))

    def step(t, carry):
        activate(2 * t + 2)

        @pl.when(t < rows // depth - 1)
        def _():
            activate(2 * t + 3)

        first = depth * t
        rhs = jnp.concatenate(
            [
                jnp.concatenate([pad[first + dy + k] for k in range(depth)], axis=1)
                for dy in range(3)
            ],
            axis=0,
        )
        y = []
        for dx in range(3):
            lhs = jnp.concatenate([ws[3 * dy + dx] for dy in range(3)], axis=1)
            y.append(jnp.dot(lhs, rhs, preferred_element_type=F32))
        for k in range(depth):
            span = slice(k * width, (k + 1) * width)
            total = from_left(y[0][:, span]) + y[1][:, span] + from_right(y[2][:, span])
            block = xl[first + k].astype(F32) + total
            out_ref[first + k] = jnp.where(first + k < length, block, 0.0).astype(BF16)
        return carry

    lax.fori_loop(0, rows // depth, step, 0)

    for copy in img_copies:
        copy.wait_recv()
    st_all[0] = st_strip[...]
    image = jnp.zeros((8, LANES), F32)
    for i in range(n_strip):
        image = image + st_all[lax.rem(strip - i + n_strip, n_strip)]
    stat_ref[...] = image / total_count

    for copy in sends:
        copy.wait_send()

    def drain(slot, carry):
        for kind in range(1, 2 + n_chips - 1):
            row_copy(slot, kind, partner, me).wait_send()
        return carry

    def drain_forward(slot, carry):
        for kind in range(1 + n_chips, 2 * n_chips):
            row_copy(slot, kind, partner, me).wait_send()
        return carry

    lax.fori_loop(1, rows + 1, drain, 0)
    lax.fori_loop(0, slots, drain_forward, 0)


def upsample_kernel(block_ref, stat_ref, out_ref, mean_ref, square_ref):
    depth, _, width = block_ref.shape
    source = lax.broadcasted_iota(jnp.int32, (width, 2 * width), 0)
    target = lax.broadcasted_iota(jnp.int32, (width, 2 * width), 1) // 2
    twice = (target == source).astype(F32).astype(BF16)
    for r in range(depth):
        wide = jnp.dot(block_ref[r], twice, preferred_element_type=F32).astype(BF16)
        out_ref[2 * r] = wide
        out_ref[2 * r + 1] = wide
    groups = mean_ref.shape[1]
    mean_ref[...] = stat_ref[0:1, 0:groups]
    square_ref[...] = stat_ref[1:2, 0:groups]


def per_device(
    n_strip,
    n_chan,
    activations,
    weight,
    gamma,
    beta,
    group_map,
    lengths,
    stale_edges,
    stale_mean,
    stale_square,
    old_mean,
    old_square,
):
    rows, width, local_c = activations.shape
    channels = weight.shape[1]
    groups = stale_mean.shape[0]
    slots = rows + 2
    n_chips = n_chan // 2
    kinds = 2 * n_chips
    total_count = float(n_strip * (3 * rows // 4) * width * (channels // groups))
    vmem = pl.BlockSpec(memory_space=pltpu.VMEM)
    hbm = pl.BlockSpec(memory_space=pl.ANY)
    dma = pltpu.SemaphoreType.DMA
    block, stat = pl.pallas_call(
        functools.partial(conv_kernel, n_strip, n_chan, total_count),
        out_shape=(
            jax.ShapeDtypeStruct((rows, local_c, width), BF16),
            jax.ShapeDtypeStruct((8, LANES), F32),
        ),
        in_specs=[hbm, hbm, vmem, vmem, vmem, pl.BlockSpec(memory_space=pltpu.SMEM), hbm,
                  vmem, vmem, vmem, vmem],
        out_specs=(vmem, vmem),
        scratch_shapes=[
            pltpu.VMEM((rows, local_c, width), BF16),
            pltpu.VMEM((2, local_c, width), BF16),
            pltpu.VMEM((9, local_c, channels), BF16),
            pltpu.VMEM((n_chan, slots, local_c, width), BF16),
            pltpu.VMEM((slots + 1, channels, width), BF16),
            pltpu.VMEM((8, LANES), F32),
            pltpu.VMEM((n_chan, 8, LANES), F32),
            pltpu.VMEM((8, LANES), F32),
            pltpu.VMEM((n_strip, 8, LANES), F32),
            pltpu.VMEM((2, channels, width), F32),
            dma((3,)),
            dma((3,)),
            dma((kinds, slots)),
            dma((kinds, slots)),
            dma((2, 1 + n_chips)),
            dma((n_chan,)),
            dma((n_chan,)),
            dma((n_strip,)),
            dma((n_strip,)),
        ],
        compiler_params=pltpu.CompilerParams(
            collective_id=0, has_side_effects=True, vmem_limit_bytes=56 * 2**20
        ),
        name="conv",
    )(
        jnp.transpose(activations, (0, 2, 1)),
        jnp.transpose(weight, (0, 2, 1)),
        gamma,
        beta,
        group_map,
        lengths,
        jnp.transpose(stale_edges, (0, 2, 1)),
        stale_mean.reshape(1, groups),
        stale_square.reshape(1, groups),
        old_mean,
        old_square,
    )
    whole = pl.BlockSpec((1, groups), lambda r: (0, 0))
    upsampled, mean, square = pl.pallas_call(
        upsample_kernel,
        grid=(rows // 2,),
        out_shape=(
            jax.ShapeDtypeStruct((2 * rows, local_c, 2 * width), BF16),
            jax.ShapeDtypeStruct((1, groups), F32),
            jax.ShapeDtypeStruct((1, groups), F32),
        ),
        in_specs=[
            pl.BlockSpec((2, local_c, width), lambda r: (r, 0, 0)),
            pl.BlockSpec((8, LANES), lambda r: (0, 0)),
        ],
        out_specs=(pl.BlockSpec((4, local_c, 2 * width), lambda r: (r, 0, 0)), whole, whole),
        name="upsample",
    )(block, stat)
    upsampled = jnp.transpose(upsampled, (0, 2, 1))
    return upsampled, mean.reshape(groups), square.reshape(groups)


def solution(mesh):
    in_specs = (
        P("strip", None, "chan"),
        P(None, None, "chan"),
        P(),
        P(),
        P(),
        P("strip"),
        P("strip", None, "chan"),
        P(),
        P(),
        P("strip", None),
        P("strip", None),
    )
    out_specs = (P("strip", None, "chan"), P(), P())
    body = functools.partial(per_device, mesh.shape["strip"], mesh.shape["chan"])
    return jax.shard_map(
        body, mesh=mesh, in_specs=in_specs, out_specs=out_specs, check_vma=False
    )
```

time: 76.7 us -> 44.8 us (0.58)
  local copies, waits for them, and re-layouts: 25.2 us -> 0 us
  Pallas kernels: 48.7 us -> 42.7 us
    unnamed x4 -> x0, local copies, waits for them, and re-layouts: 21.4 us -> none
    reshape x3 -> x0, local copies, waits for them, and re-layouts: 3.87 us -> none  [the longest x1 1.3 us: per_device(): gamma.reshape(1, channels)]
    pallas_call x1, Pallas kernels: 42.4 us -> 38.7 us  [per_device(): pl.pallas_call(functools.partial(conv_kernel, n_strip, n_chan, total_coun...]
    pallas_call x1, Pallas kernels: 6.22 us -> 4.01 us  [per_device(): pl.pallas_call(upsample_kernel, grid=(rows // 2,), out_shape=(jax.ShapeDt...]
where the time goes in v2:
time: 44.8 us; the launch traced here: 44 us
  Pallas kernels  42.7 us (95%)
  between operations  1.29 us (3%)
    pallas_call x1, Pallas kernels, per_device(): pl.pallas_call(functools.partial(conv_kernel, n_strip, n_chan, total_coun...  38.7 us
    pallas_call x1, Pallas kernels, per_device(): pl.pallas_call(upsample_kernel, grid=(rows // 2,), out_shape=(jax.ShapeDt...  4.01 us

profile of v2, /device:TPU:0, one launch (start us, length us, event | category | flops | bytes accessed | tf_op | source)
XLA Modules:
  0.0 44.0 jit_solution(17542515280597341002)
XLA Ops:
  1.3 38.7 %conv.1 = (bf16[8,320,128]{2,1,0:T(8,128)(2,1)}, f32[8,128]{1,0:T(8,128)}) custom-call(bf16[8,320,128]{2,1,0:T(8,128)(2,1)} %bitcast.9, bf16[9,320,1280]{2,1,0:T(8,128)(2,1)} %bitcast.8, f32[1280]{0:T(1024)} %gamma_ref.1, f32[1280]{0:T(1024)} %beta_ref.1, s32[1280]{0:T(1024)} %map_ref.1, s32[1]{0:T(128)S(6)} %copy.14.len_ref, bf16[2,320,128]{2,1,0:T(8,128)(2,1)} %bitcast.10, ...), custom_call_target="tpu_custom_call" | custom-call | tf_op jit(solution)/shard_map/conv/pallas_call | solution.py:347
  40.0 4.0 %upsample.1 = (bf16[16,320,256]{2,1,0:T(8,128)(2,1)}, f32[1,32]{1,0:T(1,128)}, f32[1,32]{1,0:T(1,128)}) custom-call(bf16[8,320,128]{2,1,0:T(8,128)(2,1)} %get-tuple-element.8.block_ref, f32[8,128]{1,0:T(8,128)} %get-tuple-element.9.stat_ref), custom_call_target="tpu_custom_call" | custom-call | tf_op jit(solution)/shard_map/upsample/pallas_call | solution.py:395

commit v3 on v2

--- a/solution.py
+++ b/solution.py
@@ -12,6 +12,8 @@
 F32 = jnp.float32
 BF16 = jnp.bfloat16
 LANES = 128
+CHUNK = 64
+WINDOW = 5
 
 
 def spread(row):
@@ -103,17 +105,35 @@
             greeted += 1
 
     e_copy.wait()
+    pl.semaphore_wait(barrier, greeted)
+
+    sends = []
+
+    def send(src, dst, s_sem, r_sem, device):
+        copy = pltpu.make_async_remote_copy(
+            src_ref=src, dst_ref=dst, send_sem=s_sem, recv_sem=r_sem,
+            device_id=device, device_id_type=MESH,
+        )
+        copy.start()
+        sends.append(copy)
+        return copy
+
+    for k, slot, side in ((1, 0, up), (0, slots - 1, down)):
+        for kind, c in enumerate([me, partner] + others):
+            send(el.at[k], ga.at[me, slot], edge_send.at[k, kind],
+                 recv_sem.at[kind, slot], (side, c))
+
     x_copy.wait()
-
-    def row_sums(r, carry):
-        one, two = carry
-        value = jnp.where(r < length, xl[r].astype(F32), 0.0)
-        return one + value, two + value * value
-
-    zero = jnp.zeros((local_c, width), F32)
-    one, two = lax.fori_loop(0, rows, row_sums, (zero, zero))
-    one = jnp.sum(one, axis=1, keepdims=True)
-    two = jnp.sum(two, axis=1, keepdims=True)
+    sums_one, sums_two = [], []
+    for at in range(0, local_c, CHUNK):
+        one = two = jnp.zeros((CHUNK, width), F32)
+        for r in range(rows):
+            value = jnp.where(r < length, xl[r, pl.ds(at, CHUNK)].astype(F32), 0.0)
+            one, two = one + value, two + value * value
+        sums_one.append(jnp.sum(one, axis=1, keepdims=True))
+        sums_two.append(jnp.sum(two, axis=1, keepdims=True))
+    one = jnp.concatenate(sums_one, axis=0)
+    two = jnp.concatenate(sums_two, axis=0)
     gmap = jnp.broadcast_to(map_ref[...].reshape(1, channels).astype(F32), (8, channels))
     own_map = pltpu.roll(gmap, lax.rem(channels - me * local_c, channels), 1)[0:1]
     blocks = -(-local_c // LANES)
@@ -128,20 +148,6 @@
     ).astype(F32)
     sub8 = lax.broadcasted_iota(jnp.int32, (8, LANES), 0)
     st_out[...] = jnp.where(sub8 == 0, row_one, jnp.where(sub8 == 1, row_two, 0.0))
-    g_copy.wait()
-    pl.semaphore_wait(barrier, greeted)
-
-    sends = []
-
-    def send(src, dst, s_sem, r_sem, device):
-        copy = pltpu.make_async_remote_copy(
-            src_ref=src, dst_ref=dst, send_sem=s_sem, recv_sem=r_sem,
-            device_id=device, device_id_type=MESH,
-        )
-        copy.start()
-        sends.append(copy)
-        return copy
-
     stat_copies = []
     for d in range(1, n_chan):
         peer = lax.rem(me + d, n_chan)
@@ -149,11 +155,6 @@
             send(st_out, st_chan.at[d], stat_send.at[d], stat_recv.at[d], (strip, peer))
         )
 
-    for k, slot, side in ((1, 0, up), (0, slots - 1, down)):
-        for kind, c in enumerate([me, partner] + others):
-            send(el.at[k], ga.at[me, slot], edge_send.at[k, kind],
-                 recv_sem.at[kind, slot], (side, c))
-
     def row_copy(slot, kind, c, chan):
         return pltpu.make_async_remote_copy(
             src_ref=ga.at[chan, slot], dst_ref=ga.at[chan, slot],
@@ -161,13 +162,28 @@
             device_id=(strip, c), device_id_type=MESH,
         )
 
+    g_copy.wait()
     def start_row(slot, carry):
         for kind, c in enumerate(others):
             row_copy(slot, 2 + kind, c, me).start()
         row_copy(slot, 1, partner, me).start()
         return carry
 
-    lax.fori_loop(1, rows + 1, start_row, 0)
+    lax.fori_loop(1, min(WINDOW, rows) + 1, start_row, 0)
+
+    def forward(slot):
+        for kind, c in enumerate(sources):
+            row_copy(slot, 2 + kind, c, c).wait_recv()
+            row_copy(slot, 1 + n_chips + kind, partner, c).start()
+
+    def arrive(slot):
+        row_copy(slot, 1, partner, partner).wait_recv()
+        for kind, c in enumerate(sources):
+            far = c // 2 * 2 + (1 - core)
+            row_copy(slot, 1 + n_chips + kind, partner, far).wait_recv()
+
+    for slot in (0, slots - 1):
+        forward(slot)
 
     for copy in stat_copies:
         copy.wait_recv()
@@ -205,19 +221,6 @@
             send(st_strip, st_all.at[d], img_send.at[d], img_recv.at[d], (peer, me))
         )
 
-    def forward(slot):
-        for kind, c in enumerate(sources):
-            row_copy(slot, 2 + kind, c, c).wait_recv()
-            row_copy(slot, 1 + n_chips + kind, partner, c).start()
-
-    def arrive(slot):
-        row_copy(slot, 1, partner, partner).wait_recv()
-        for kind, c in enumerate(sources):
-            far = c // 2 * 2 + (1 - core)
-            row_copy(slot, 1 + n_chips + kind, partner, far).wait_recv()
-
-    for slot in (0, slots - 1):
-        forward(slot)
     for slot in (0, slots - 1):
         row_copy(slot, 0, me, me).wait_recv()
         arrive(slot)
@@ -230,18 +233,26 @@
         pad[slots, span] = below.astype(BF16)
         pad[slots - 1, span] = jnp.where(length + 1 == slots - 1, below, 0.0).astype(BF16)
 
+    def relay(slot):
+        forward(slot)
+
+        @pl.when(slot + WINDOW <= rows)
+        def _():
+            start_row(slot + WINDOW, 0)
+
     def activate(slot):
-        forward(slot)
         arrive(slot)
         for c in range(n_chan):
-            span = pl.ds(c * local_c, local_c)
-            h = ga[c, slot].astype(F32) * affine[0, span] + affine[1, span]
-            act = jnp.where(slot - 1 < length, h + h * jnp.tanh(h), 0.0)
-            below = pad[slots, span].astype(F32)
-            pad[slot, span] = jnp.where(slot == length + 1, below, act).astype(BF16)
+            for at in range(0, local_c, CHUNK):
+                span = pl.ds(c * local_c + at, CHUNK)
+                h = ga[c, slot, pl.ds(at, CHUNK)].astype(F32) * affine[0, span] + affine[1, span]
+                act = jnp.where(slot - 1 < length, h + h * jnp.tanh(h), 0.0)
+                below = pad[slots, span].astype(F32)
+                pad[slot, span] = jnp.where(slot == length + 1, below, act).astype(BF16)
 
     for copy in w_copies:
         copy.wait()
+    relay(1)
     activate(1)
     depth = 2
     place = lane_iota((local_c, width))
@@ -253,9 +264,16 @@
         return jnp.where(place == width - 1, 0.0, pltpu.roll(y, width - 1, 1))
 
     def step(t, carry):
+        more = t < rows // depth - 1
+        relay(2 * t + 2)
+
+        @pl.when(more)
+        def _():
+            relay(2 * t + 3)
+
         activate(2 * t + 2)
 
-        @pl.when(t < rows // depth - 1)
+        @pl.when(more)
         def _():
             activate(2 * t + 3)
 
@@ -394,17 +412,17 @@
     whole = pl.BlockSpec((1, groups), lambda r: (0, 0))
     upsampled, mean, square = pl.pallas_call(
         upsample_kernel,
-        grid=(rows // 2,),
+        grid=(rows // 4,),
         out_shape=(
             jax.ShapeDtypeStruct((2 * rows, local_c, 2 * width), BF16),
             jax.ShapeDtypeStruct((1, groups), F32),
             jax.ShapeDtypeStruct((1, groups), F32),
         ),
         in_specs=[
-            pl.BlockSpec((2, local_c, width), lambda r: (r, 0, 0)),
+            pl.BlockSpec((4, local_c, width), lambda r: (r, 0, 0)),
             pl.BlockSpec((8, LANES), lambda r: (0, 0)),
         ],
-        out_specs=(pl.BlockSpec((4, local_c, 2 * width), lambda r: (r, 0, 0)), whole, whole),
+        out_specs=(pl.BlockSpec((8, local_c, 2 * width), lambda r: (r, 0, 0)), whole, whole),
         name="upsample",
     )(block, stat)
     upsampled = jnp.transpose(upsampled, (0, 2, 1))

time: 44.8 us -> 40.2 us (0.90); the launches traced: 44 us -> 40 us
  Pallas kernels: 42.7 us -> 38.7 us
    pallas_call x1, Pallas kernels: 38.7 us -> 35.9 us  [per_device(): pl.pallas_call(functools.partial(conv_kernel, n_strip, n_chan, total_coun...]
    pallas_call x1, Pallas kernels: 4.01 us -> 2.8 us  [per_device(): pl.pallas_call(upsample_kernel, grid=(rows // 4,), out_shape=(jax.ShapeDt...]
where the time goes in v3:
time: 40.2 us; the launch traced here: 40 us
  Pallas kernels  38.7 us (96%)
  between operations  1.29 us (3%)
    pallas_call x1, Pallas kernels, per_device(): pl.pallas_call(functools.partial(conv_kernel, n_strip, n_chan, total_coun...  35.9 us
    pallas_call x1, Pallas kernels, per_device(): pl.pallas_call(upsample_kernel, grid=(rows // 4,), out_shape=(jax.ShapeDt...  2.8 us

profile of v3, /device:TPU:0, one launch (start us, length us, event | category | flops | bytes accessed | tf_op | source)
XLA Modules:
  0.0 40.0 jit_solution(8211039277504149063)
XLA Ops:
  1.3 35.9 %conv.1 = (bf16[8,320,128]{2,1,0:T(8,128)(2,1)}, f32[8,128]{1,0:T(8,128)}) custom-call(bf16[8,320,128]{2,1,0:T(8,128)(2,1)} %bitcast.9, bf16[9,320,1280]{2,1,0:T(8,128)(2,1)} %bitcast.8, f32[1280]{0:T(1024)} %gamma_ref.1, f32[1280]{0:T(1024)} %beta_ref.1, s32[1280]{0:T(1024)} %map_ref.1, s32[1]{0:T(128)S(6)} %copy.14.len_ref, bf16[2,320,128]{2,1,0:T(8,128)(2,1)} %bitcast.10, ...), custom_call_target="tpu_custom_call" | custom-call | tf_op jit(solution)/shard_map/conv/pallas_call | solution.py:365
  37.2 2.8 %upsample.1 = (bf16[16,320,256]{2,1,0:T(8,128)(2,1)}, f32[1,32]{1,0:T(1,128)}, f32[1,32]{1,0:T(1,128)}) custom-call(bf16[8,320,128]{2,1,0:T(8,128)(2,1)} %get-tuple-element.8.block_ref, f32[8,128]{1,0:T(8,128)} %get-tuple-element.9.stat_ref), custom_call_target="tpu_custom_call" | custom-call | tf_op jit(solution)/shard_map/upsample/pallas_call | solution.py:413
